TPU v7x, 32 devices: a whole 2x2x4 slice. The times are simulated.
32 devices in a mesh: row: 8 (over z, x), col: 4 (over y, core).
Axes of the slice: x: 2, y: 2, z: 4, core: 2. Of those that a mesh axis runs over, the one named last changes fastest.
Arguments:
- hub_seeds: bfloat16 [192, 64, 128], P('row'), may hold values from -6 to 6
- tile_blocks: bfloat16 [8192, 128, 128], P(('row', 'col')), may hold values from -8 to 8
- tile_rows: int32 [8192], P(('row', 'col')), may hold values from 0 to 127, as said below
- tile_cols: int32 [8192], P(('row', 'col')), may hold values from 0 to 127, as said below
- tile_count: int32 [32], P(('row', 'col')), may hold values from 64 to 256, as said below
- row_blocks: int32 [8], replicated, may hold values from 8 to 24, as said below
Outputs:
- authority: bfloat16 [128, 64, 128], P(('row', 'col'))
- hub_scores: bfloat16 [192, 64, 128], P('row')
Inputs may be any that keep to these rules, and one draw needn't show every extreme that they name: Row range r covers row blocks starts[r] to starts[r] + row_blocks[r] - 1, the ranges in order and together all 128 blocks; the longest range has exactly 24 blocks in every draw. `tile_rows`: every tile of a device lies in the row range of the device's row index; no pair of row block and column block repeats within a device. `tile_cols`: A device with column index c holds only column blocks b with (b // 4) % 4 == c. The live tiles of a device are its first tile_count slots; some device has all 256 slots live in every draw.
All inputs are finite; a program needn't handle non-finite values.
Results may differ from a plain program's by a relative error of at most 0.02.
Values may be sent and summed in bfloat16 or wider, within the bound.
A program may use at most 192 MiB of HBM per device.

v0:
```python
import jax
import jax.numpy as jnp
from jax import lax
from jax.sharding import PartitionSpec as P

ITERS = 2
RB_DEV = 16


def local(hub_seeds, tile_blocks, tile_rows, tile_cols, tile_count, row_blocks):
    own_row = lax.axis_index("row")
    row_devs = lax.axis_size("row")
    col_devs = lax.axis_size("col")
    slot_count = hub_seeds.shape[0]
    tile_side = tile_blocks.shape[1]
    tile_slots = tile_blocks.shape[0]
    group_len = RB_DEV // col_devs
    set_blocks = group_len * row_devs
    host_count = RB_DEV * row_devs * tile_side
    span_length = row_blocks[own_row]
    before = jnp.arange(row_devs, dtype=jnp.int32) < own_row
    first_block = jnp.sum(jnp.where(before, row_blocks, 0))
    live_tile = jnp.arange(tile_slots, dtype=jnp.int32) < tile_count[0]
    row_slot = jnp.where(live_tile, tile_rows - first_block, slot_count)
    col_slot = jnp.where(
        live_tile,
        tile_cols // group_len // col_devs * group_len + tile_cols % group_len,
        set_blocks,
    )
    row_pick = jnp.clip(row_slot, 0, slot_count - 1)
    col_pick = jnp.clip(col_slot, 0, set_blocks - 1)
    usable = jnp.arange(slot_count, dtype=jnp.int32) < span_length
    hub_now = jnp.where(usable[:, None, None], hub_seeds, jnp.zeros_like(hub_seeds))
    authority = None
    for iteration in range(ITERS):
        picked = jnp.take(hub_now, row_pick, axis=0, mode="clip")
        products = jnp.einsum(
            "tkr,trc->tkc", picked, tile_blocks, preferred_element_type=jnp.float32
        )
        set_terms = jax.ops.segment_sum(products, col_slot, num_segments=set_blocks, mode="drop")
        raw_set = lax.psum(set_terms.astype(jnp.bfloat16), "row").astype(jnp.float32)
        squares = lax.psum(jnp.sum(raw_set * raw_set, axis=(0, 2)), "col")
        factor = 1.0 / jnp.sqrt(squares / host_count + 1.0)
        column_set = (raw_set * factor[None, :, None]).astype(jnp.bfloat16)
        authority = lax.dynamic_slice_in_dim(column_set, own_row * group_len, group_len, 0)
        picked_cols = jnp.take(column_set, col_pick, axis=0, mode="clip")
        back_products = jnp.einsum(
            "tkc,trc->tkr", picked_cols, tile_blocks, preferred_element_type=jnp.float32
        )
        hub_terms = jax.ops.segment_sum(
            back_products, row_slot, num_segments=slot_count, mode="drop"
        )
        raw_hub = lax.psum(hub_terms.astype(jnp.bfloat16), "col").astype(jnp.float32)
        squares = lax.psum(jnp.sum(raw_hub * raw_hub, axis=(0, 2)), "row")
        factor = 1.0 / jnp.sqrt(squares / host_count + 1.0)
        hub_now = (raw_hub * factor[None, :, None]).astype(jnp.bfloat16)
    return (authority, hub_now)


def solution(mesh):
    return jax.shard_map(
        local,
        mesh=mesh,
        in_specs=(
            P("row", None, None),
            P(("row", "col"), None, None),
            P(("row", "col")),
            P(("row", "col")),
            P(("row", "col")),
            P(),
        ),
        out_specs=(P(("row", "col"), None, None), P("row", None, None)),
        check_vma=False,
    )
```

profile of v0, /device:TPU:0, one launch (start us, length us, event | category | flops | bytes accessed | tf_op | source)
XLA Modules:
  0.0 463.2 jit_solution(11632191388393047059)
XLA Ops:
  7.2 1.3 fusion.10
  8.5 1.2 dynamic_slice.6
  11.0 1.4 broadcast_clamp_fusion
  12.4 1.1 broadcast_select_fusion
  13.5 3.1 gather_fusion
  16.6 10.2 %fusion.12 = f32[256,64,128]{2,1,0:T(8,128)} fusion(bf16[256,64,128]{2,1,0:T(8,128)(2,1)} %gather_fusion, bf16[256,128,128]{2,1,0:T(8,128)(2,1)} %param.7), kind=kOutput, calls=%fused_computation.50 | convolution fusion | flops 536870912 | bytes 20971520 | tf_op jit(solution)/shard_map/tkr,trc->tkc/dot_general | solution.py:37
  26.9 26.3 %scatter_fusion = f32[32,64,128]{2,1,0:T(8,128)S(1)} fusion(f32[32,64,128]{2,1,0:T(8,128)S(1)} %broadcast.40.clone, s32[256]{0:T(256)S(1)} %get-tuple-element.3, f32[256,64,128]{2,1,0:T(8,128)} %fusion.12), kind=kCustom, calls=%fused_computation.4 | custom fusion | flops 2097152 | bytes 25166848 | tf_op jit(solution)/shard_map/scatter-add | solution.py:40
  54.2 75.3 %all-reduce.5.cloned.1.call-done = bf16[32,64,128]{2,1,0:T(8,128)(2,1)} async-done(((bf16[32,64,128]{2,1,0:T(8,128)(2,1)}), bf16[32,64,128]{2,1,0:T(8,128)(2,1)}) %all-reduce.5.cloned.1.call-update) | async-done | bytes 524304 | tf_op jit(solution)/shard_map/psum | solution.py:41
  129.5 1.3 fusion
  130.8 5.7 %psum.57 = f32[64]{0:T(128)S(1)} all-reduce(f32[64]{0:T(128)S(1)} %fusion), channel_id=1, replica_groups=mesh['row'=8,'col'=4] {'col'}, use_global_device_ids=true, to_apply=%region_4.5 | all-reduce | flops 64 | bytes 512 | tf_op jit(solution)/shard_map/psum | solution.py:42
  136.5 1.3 fusion.1
  137.7 3.1 gather_fusion.1
  140.8 13.7 %fusion.13 = f32[256,64,128]{2,1,0:T(8,128)} fusion(bf16[256,64,128]{2,1,0:T(8,128)(2,1)} %gather_fusion.1, bf16[256,128,128]{2,1,0:T(8,128)(2,1)} %param.7), kind=kOutput, calls=%fused_computation.51 | convolution fusion | flops 536870912 | bytes 20971520 | tf_op jit(solution)/shard_map/tkc,trc->tkr/dot_general | solution.py:47
  154.6 26.3 %scatter_fusion.1 = f32[24,64,128]{2,1,0:T(8,128)S(1)} fusion(f32[24,64,128]{2,1,0:T(8,128)S(1)} %broadcast.42.clone, s32[256]{0:T(256)S(1)} %get-tuple-element.7, f32[256,64,128]{2,1,0:T(8,128)} %fusion.13), kind=kCustom, calls=%fused_computation.5 | custom fusion | flops 2097152 | bytes 25166848 | tf_op jit(solution)/shard_map/scatter-add | solution.py:50
  181.8 32.2 %all-reduce.7.cloned.1.call-done = bf16[24,64,128]{2,1,0:T(8,128)(2,1)} async-done(((bf16[24,64,128]{2,1,0:T(8,128)(2,1)}), bf16[24,64,128]{2,1,0:T(8,128)(2,1)}) %all-reduce.7.cloned.1.call-update) | async-done | bytes 393232 | tf_op jit(solution)/shard_map/psum | solution.py:53
  214.1 1.2 fusion.4
  215.2 21.5 %psum.59 = f32[64]{0:T(128)S(1)} all-reduce(f32[64]{0:T(128)S(1)} %fusion.4), channel_id=1, replica_groups=mesh['row'=8,'col'=4] {'row'}, use_global_device_ids=true, to_apply=%region_8.9 | all-reduce | flops 64 | bytes 512 | tf_op jit(solution)/shard_map/psum | solution.py:54
  236.8 1.2 fusion.5
  238.0 3.1 gather_fusion.2
  241.0 10.2 %fusion.14 = f32[256,64,128]{2,1,0:T(8,128)} fusion(bf16[256,64,128]{2,1,0:T(8,128)(2,1)} %gather_fusion.2, bf16[256,128,128]{2,1,0:T(8,128)(2,1)} %param.7), kind=kOutput, calls=%fused_computation.52 | convolution fusion | flops 536870912 | bytes 20971520 | tf_op jit(solution)/shard_map/tkr,trc->tkc/dot_general | solution.py:37
  251.4 26.3 %scatter_fusion.2 = f32[32,64,128]{2,1,0:T(8,128)S(1)} fusion(f32[32,64,128]{2,1,0:T(8,128)S(1)} %broadcast.40, s32[256]{0:T(256)S(1)} %get-tuple-element.3, f32[256,64,128]{2,1,0:T(8,128)} %fusion.14), kind=kCustom, calls=%fused_computation.6 | custom fusion | flops 2097152 | bytes 25166848 | tf_op jit(solution)/shard_map/scatter-add | solution.py:40
  278.6 69.0 %all-reduce.9.cloned.1.call-done = bf16[32,64,128]{2,1,0:T(8,128)(2,1)} async-done(((bf16[32,64,128]{2,1,0:T(8,128)(2,1)}), bf16[32,64,128]{2,1,0:T(8,128)(2,1)}) %all-reduce.9.cloned.1.call-update) | async-done | bytes 524304 | tf_op jit(solution)/shard_map/psum | solution.py:41
  347.7 1.3 fusion.2
  348.9 5.7 %psum.61 = f32[64]{0:T(128)S(1)} all-reduce(f32[64]{0:T(128)S(1)} %fusion.2), channel_id=1, replica_groups=mesh['row'=8,'col'=4] {'col'}, use_global_device_ids=true, to_apply=%region_12.13 | all-reduce | flops 64 | bytes 512 | tf_op jit(solution)/shard_map/psum | solution.py:42
  354.6 1.3 fusion.3
  355.9 3.1 gather_fusion.3
  358.9 13.7 %fusion.15 = f32[256,64,128]{2,1,0:T(8,128)} fusion(bf16[256,64,128]{2,1,0:T(8,128)(2,1)} %gather_fusion.3, bf16[256,128,128]{2,1,0:T(8,128)(2,1)} %param.7), kind=kOutput, calls=%fused_computation.53 | convolution fusion | flops 536870912 | bytes 20971520 | tf_op jit(solution)/shard_map/tkc,trc->tkr/dot_general | solution.py:47
  372.7 26.3 %scatter_fusion.3 = f32[24,64,128]{2,1,0:T(8,128)S(1)} fusion(f32[24,64,128]{2,1,0:T(8,128)S(1)} %broadcast.42, s32[256]{0:T(256)S(1)} %get-tuple-element.7, f32[256,64,128]{2,1,0:T(8,128)} %fusion.15), kind=kCustom, calls=%fused_computation.7 | custom fusion | flops 2097152 | bytes 25166848 | tf_op jit(solution)/shard_map/scatter-add | solution.py:50
  400.5 31.6 %all-reduce.11.cloned.1.call-done = bf16[24,64,128]{2,1,0:T(8,128)(2,1)} async-done(((bf16[24,64,128]{2,1,0:T(8,128)(2,1)}), bf16[24,64,128]{2,1,0:T(8,128)(2,1)}) %all-reduce.11.cloned.1.call-update) | async-done | bytes 393232 | tf_op jit(solution)/shard_map/psum | solution.py:53
  432.2 1.2 fusion.6
  433.4 21.4 %psum.63 = f32[64]{0:T(128)S(1)} all-reduce(f32[64]{0:T(128)S(1)} %fusion.6), channel_id=1, replica_groups=mesh['row'=8,'col'=4] {'row'}, use_global_device_ids=true, to_apply=%region_16.17 | all-reduce | flops 64 | bytes 512 | tf_op jit(solution)/shard_map/psum | solution.py:54
  454.7 1.9 fusion.7
  (24 shorter events, 5.3 us)
Async XLA Ops:
  7.2 122.4 %all-reduce.5.cloned.1.call-start = ((), (), s32[]{:S(2)}) async-start(), calls=%async_computation | async-start | bytes 1048576 | tf_op jit(solution)/shard_map/psum | solution.py:41
  54.2 159.9 %all-reduce.7.cloned.1.call-start = ((), (), s32[]{:S(2)}) async-start(), calls=%async_computation.1 | async-start | bytes 786432 | tf_op jit(solution)/shard_map/psum | solution.py:53
  181.8 165.9 %all-reduce.9.cloned.1.call-start = ((), (), s32[]{:S(2)}) async-start(), calls=%async_computation.2 | async-start | bytes 1048576 | tf_op jit(solution)/shard_map/psum | solution.py:41
  278.6 153.6 %all-reduce.11.cloned.1.call-start = ((), (), s32[]{:S(2)}) async-start(), calls=%async_computation.3 | async-start | bytes 786432 | tf_op jit(solution)/shard_map/psum | solution.py:53
Sparse Core Ops, SparseCore 0:
  54.3 75.2 all-reduce.4
  181.9 32.1 all-reduce.6
  278.7 68.9 all-reduce.8
  400.0 32.1 all-reduce.10
where the time goes:
time: 467 us; the launch traced here: 463 us
  waiting for transfers between devices  208 us (45%)
  other arithmetic  124 us (27%)
  blocking collectives  54.2 us (12%)
  matrix products  47.9 us (10%)
  between operations  14.6 us (3%)
  local copies, waits for them, and re-layouts  14.5 us (3%)
    psum x2, waiting for transfers between devices, local(): lax.psum(set_terms.astype(jnp.bfloat16), 'row').astype(jnp.float32)  144 us
    psum x2, waiting for transfers between devices, local(): lax.psum(hub_terms.astype(jnp.bfloat16), 'col').astype(jnp.float32)  63.9 us
    scatter-add x2, other arithmetic, local(): jax.ops.segment_sum(back_products, row_slot, num_segments=slot_count, mod...  52.6 us
    scatter-add x2, other arithmetic, local(): jax.ops.segment_sum(products, col_slot, num_segments=set_blocks, mode='dr...  52.6 us
    psum x2, blocking collectives, local(): squares = lax.psum(jnp.sum(raw_hub * raw_hub, axis=(0, 2)), 'row')  42.9 us
    dot_general x2, matrix products, local(): jnp.einsum('tkc,trc->tkr', picked_cols, tile_blocks, preferred_element_ty...  27.5 us
    dot_general x2, matrix products, local(): jnp.einsum('tkr,trc->tkc', picked, tile_blocks, preferred_element_type=jn...  20.4 us
    psum x2, blocking collectives, local(): squares = lax.psum(jnp.sum(raw_set * raw_set, axis=(0, 2)), 'col')  11.3 us
  transfers between devices with their start and end apart: 4, of which 4 were waited for; matrix products, arithmetic and copies ran while one was open for 0% of the time, Pallas kernels for 0%

commit v1 on v0

--- a/solution.py
+++ b/solution.py
@@ -38,7 +38,9 @@
             "tkr,trc->tkc", picked, tile_blocks, preferred_element_type=jnp.float32
         )
         set_terms = jax.ops.segment_sum(products, col_slot, num_segments=set_blocks, mode="drop")
-        raw_set = lax.psum(set_terms.astype(jnp.bfloat16), "row").astype(jnp.float32)
+        raw_set = jnp.sum(lax.all_gather(set_terms.astype(jnp.bfloat16), "row"), axis=0).astype(
+            jnp.float32
+        )
         squares = lax.psum(jnp.sum(raw_set * raw_set, axis=(0, 2)), "col")
         factor = 1.0 / jnp.sqrt(squares / host_count + 1.0)
         column_set = (raw_set * factor[None, :, None]).astype(jnp.bfloat16)

time: 467 us -> 468 us (level)
    all_gather x0 -> x2, waiting for transfers between devices: none -> 145 us  [local(): lax.all_gather(set_terms.astype(jnp.bfloat16), 'row')]
    psum x2 -> x0, waiting for transfers between devices: 144 us -> none  [local(): lax.psum(set_terms.astype(jnp.bfloat16), 'row').astype(jnp.float32)]
    reduce_sum x0 -> x2, other arithmetic: none -> 6.19 us  [local(): jnp.sum(lax.all_gather(set_terms.astype(jnp.bfloat16), 'row'), axis=0)]
where the time goes in v1:
time: 468 us; the launch traced here: 464 us
  waiting for transfers between devices  207 us (44%)
  other arithmetic  126 us (27%)
  blocking collectives  54.2 us (12%)
  matrix products  47.9 us (10%)
  between operations  14.6 us (3%)
  local copies, waits for them, and re-layouts  14.5 us (3%)
    all_gather x2, waiting for transfers between devices, local(): lax.all_gather(set_terms.astype(jnp.bfloat16), 'row')  145 us
    psum x2, waiting for transfers between devices, local(): lax.psum(hub_terms.astype(jnp.bfloat16), 'col').astype(jnp.float32)  62.6 us
    scatter-add x2, other arithmetic, local(): jax.ops.segment_sum(back_products, row_slot, num_segments=slot_count, mod...  52.6 us
    scatter-add x2, other arithmetic, local(): jax.ops.segment_sum(products, col_slot, num_segments=set_blocks, mode='dr...  52.6 us
    psum x2, blocking collectives, local(): squares = lax.psum(jnp.sum(raw_hub * raw_hub, axis=(0, 2)), 'row')  42.9 us
    dot_general x2, matrix products, local(): jnp.einsum('tkc,trc->tkr', picked_cols, tile_blocks, preferred_element_ty...  27.5 us
    dot_general x2, matrix products, local(): jnp.einsum('tkr,trc->tkc', picked, tile_blocks, preferred_element_type=jn...  20.4 us
    psum x2, blocking collectives, local(): squares = lax.psum(jnp.sum(raw_set * raw_set, axis=(0, 2)), 'col')  11.3 us
  transfers between devices with their start and end apart: 4, of which 4 were waited for; matrix products, arithmetic and copies ran while one was open for 0% of the time, Pallas kernels for 0%

profile of v1, /device:TPU:0, one launch (start us, length us, event | category | flops | bytes accessed | tf_op | source)
XLA Modules:
  0.0 464.2 jit_solution(10246737490859987426)
XLA Ops:
  7.2 1.3 fusion.10
  8.5 1.2 dynamic_slice.6
  11.0 1.4 broadcast_clamp_fusion
  12.4 1.1 broadcast_select_fusion
  13.5 3.1 gather_fusion
  16.6 10.2 %fusion.12 = f32[256,64,128]{2,1,0:T(8,128)} fusion(bf16[256,64,128]{2,1,0:T(8,128)(2,1)} %gather_fusion, bf16[256,128,128]{2,1,0:T(8,128)(2,1)} %param.7), kind=kOutput, calls=%fused_computation.50 | convolution fusion | flops 536870912 | bytes 20971520 | tf_op jit(solution)/shard_map/tkr,trc->tkc/dot_general | solution.py:37
  26.9 26.3 %scatter_fusion = f32[32,64,128]{2,1,0:T(8,128)S(1)} fusion(f32[32,64,128]{2,1,0:T(8,128)S(1)} %broadcast.40.clone, s32[256]{0:T(256)S(1)} %get-tuple-element.3, f32[256,64,128]{2,1,0:T(8,128)} %fusion.12), kind=kCustom, calls=%fused_computation.4 | custom fusion | flops 2097152 | bytes 25166848 | tf_op jit(solution)/shard_map/scatter-add | solution.py:40
  53.2 0.9 convert_element_type.40
  54.2 75.5 %all-gather.5.cloned.1.call-done = bf16[256,64,128]{2,1,0:T(8,128)(2,1)} async-done(((bf16[32,64,128]{2,1,0:T(8,128)(2,1)}), bf16[256,64,128]{2,1,0:T(8,128)(2,1)}) %all-gather.5.cloned.1.call-update) | async-done | bytes 4194320 | tf_op jit(solution)/shard_map/all_gather | solution.py:41
  129.7 3.1 reduce_sum.70
  133.0 5.7 %psum.42 = f32[64]{0:T(128)S(1)} all-reduce(f32[64]{0:T(128)S(1)} %fusion), channel_id=1, replica_groups=mesh['row'=8,'col'=4] {'col'}, use_global_device_ids=true, to_apply=%region_4.5 | all-reduce | flops 64 | bytes 512 | tf_op jit(solution)/shard_map/psum | solution.py:44
  138.9 3.1 gather_fusion.1
  142.0 13.7 %fusion.13 = f32[256,64,128]{2,1,0:T(8,128)} fusion(bf16[256,64,128]{2,1,0:T(8,128)(2,1)} %gather_fusion.1, bf16[256,128,128]{2,1,0:T(8,128)(2,1)} %param.7), kind=kOutput, calls=%fused_computation.51 | convolution fusion | flops 536870912 | bytes 20971520 | tf_op jit(solution)/shard_map/tkc,trc->tkr/dot_general | solution.py:49
  155.8 26.3 %scatter_fusion.1 = f32[24,64,128]{2,1,0:T(8,128)S(1)} fusion(f32[24,64,128]{2,1,0:T(8,128)S(1)} %broadcast.42.clone, s32[256]{0:T(256)S(1)} %get-tuple-element.7, f32[256,64,128]{2,1,0:T(8,128)} %fusion.13), kind=kCustom, calls=%fused_computation.5 | custom fusion | flops 2097152 | bytes 25166848 | tf_op jit(solution)/shard_map/scatter-add | solution.py:52
  183.0 31.6 %all-reduce.3.cloned.1.call-done = bf16[24,64,128]{2,1,0:T(8,128)(2,1)} async-done(((bf16[24,64,128]{2,1,0:T(8,128)(2,1)}), bf16[24,64,128]{2,1,0:T(8,128)(2,1)}) %all-reduce.3.cloned.1.call-update) | async-done | bytes 393232 | tf_op jit(solution)/shard_map/psum | solution.py:55
  214.6 1.2 fusion.4
  215.8 21.5 %psum.44 = f32[64]{0:T(128)S(1)} all-reduce(f32[64]{0:T(128)S(1)} %fusion.4), channel_id=1, replica_groups=mesh['row'=8,'col'=4] {'row'}, use_global_device_ids=true, to_apply=%region_8.9 | all-reduce | flops 64 | bytes 512 | tf_op jit(solution)/shard_map/psum | solution.py:56
  237.3 1.2 fusion.5
  238.5 3.1 gather_fusion.2
  241.6 10.2 %fusion.14 = f32[256,64,128]{2,1,0:T(8,128)} fusion(bf16[256,64,128]{2,1,0:T(8,128)(2,1)} %gather_fusion.2, bf16[256,128,128]{2,1,0:T(8,128)(2,1)} %param.7), kind=kOutput, calls=%fused_computation.52 | convolution fusion | flops 536870912 | bytes 20971520 | tf_op jit(solution)/shard_map/tkr,trc->tkc/dot_general | solution.py:37
  251.9 26.3 %scatter_fusion.2 = f32[32,64,128]{2,1,0:T(8,128)S(1)} fusion(f32[32,64,128]{2,1,0:T(8,128)S(1)} %broadcast.40, s32[256]{0:T(256)S(1)} %get-tuple-element.3, f32[256,64,128]{2,1,0:T(8,128)} %fusion.14), kind=kCustom, calls=%fused_computation.6 | custom fusion | flops 2097152 | bytes 25166848 | tf_op jit(solution)/shard_map/scatter-add | solution.py:40
  278.2 0.9 convert_element_type.46
  279.1 69.2 %all-gather.7.cloned.1.call-done = bf16[256,64,128]{2,1,0:T(8,128)(2,1)} async-done(((bf16[32,64,128]{2,1,0:T(8,128)(2,1)}), bf16[256,64,128]{2,1,0:T(8,128)(2,1)}) %all-gather.7.cloned.1.call-update) | async-done | bytes 4194320 | tf_op jit(solution)/shard_map/all_gather | solution.py:41
  348.3 3.1 reduce_sum.73
  351.6 5.7 %psum.45 = f32[64]{0:T(128)S(1)} all-reduce(f32[64]{0:T(128)S(1)} %fusion.2), channel_id=1, replica_groups=mesh['row'=8,'col'=4] {'col'}, use_global_device_ids=true, to_apply=%region_12.13 | all-reduce | flops 64 | bytes 512 | tf_op jit(solution)/shard_map/psum | solution.py:44
  357.5 3.1 gather_fusion.3
  360.6 13.7 %fusion.15 = f32[256,64,128]{2,1,0:T(8,128)} fusion(bf16[256,64,128]{2,1,0:T(8,128)(2,1)} %gather_fusion.3, bf16[256,128,128]{2,1,0:T(8,128)(2,1)} %param.7), kind=kOutput, calls=%fused_computation.53 | convolution fusion | flops 536870912 | bytes 20971520 | tf_op jit(solution)/shard_map/tkc,trc->tkr/dot_general | solution.py:49
  374.4 26.3 %scatter_fusion.3 = f32[24,64,128]{2,1,0:T(8,128)S(1)} fusion(f32[24,64,128]{2,1,0:T(8,128)S(1)} %broadcast.42, s32[256]{0:T(256)S(1)} %get-tuple-element.7, f32[256,64,128]{2,1,0:T(8,128)} %fusion.15), kind=kCustom, calls=%fused_computation.7 | custom fusion | flops 2097152 | bytes 25166848 | tf_op jit(solution)/shard_map/scatter-add | solution.py:52
  402.2 31.0 %all-reduce.5.cloned.1.call-done = bf16[24,64,128]{2,1,0:T(8,128)(2,1)} async-done(((bf16[24,64,128]{2,1,0:T(8,128)(2,1)}), bf16[24,64,128]{2,1,0:T(8,128)(2,1)}) %all-reduce.5.cloned.1.call-update) | async-done | bytes 393232 | tf_op jit(solution)/shard_map/psum | solution.py:55
  433.2 1.2 fusion.6
  434.4 21.4 %psum.47 = f32[64]{0:T(128)S(1)} all-reduce(f32[64]{0:T(128)S(1)} %fusion.6), channel_id=1, replica_groups=mesh['row'=8,'col'=4] {'row'}, use_global_device_ids=true, to_apply=%region_16.17 | all-reduce | flops 64 | bytes 512 | tf_op jit(solution)/shard_map/psum | solution.py:56
  455.7 1.9 fusion.7
  (26 shorter events, 4.4 us)
Async XLA Ops:
  7.2 122.5 %all-gather.5.cloned.1.call-start = ((), (), s32[]{:S(2)}) async-start(), calls=%async_computation.2 | async-start | bytes 4718592 | tf_op jit(solution)/shard_map/all_gather | solution.py:41
  54.1 160.4 %all-reduce.3.cloned.1.call-start = ((), (), s32[]{:S(2)}) async-start(), calls=%async_computation | async-start | bytes 786432 | tf_op jit(solution)/shard_map/psum | solution.py:55
  182.9 165.4 %all-gather.7.cloned.1.call-start = ((), (), s32[]{:S(2)}) async-start(), calls=%async_computation.3 | async-start | bytes 4718592 | tf_op jit(solution)/shard_map/all_gather | solution.py:41
  279.1 154.1 %all-reduce.5.cloned.1.call-start = ((), (), s32[]{:S(2)}) async-start(), calls=%async_computation.1 | async-start | bytes 786432 | tf_op jit(solution)/shard_map/psum | solution.py:55
Sparse Core Ops, SparseCore 0:
  54.3 75.3 all-gather.4
  183.1 31.4 all-reduce.2
  279.2 69.0 all-gather.6
  401.7 31.4 all-reduce.4
